TPU v7x, 16 devices: a 4x2x1 block of a 4x4x8 slice. The times are simulated.
16 devices in a mesh: dp: 2 (over y, z), tp: 8 (over x, core).
Axes of the slice: x: 4, y: 2, z: 1, core: 2. Of those that a mesh axis runs over, the one named last changes fastest.
The devices are a block of a 4x4x8 slice.
Arguments:
- x_in: bfloat16 [32, 512, 1024], P('dp', 'tp'), parts along dimension 0
- grad_y: bfloat16 [32, 512, 1024], P('dp', 'tp'), parts along dimension 0
- pad_mask: int32 [32, 512], P('dp'), parts along dimension 0
- ln1_gain: float32 [1024], replicated
- ln1_bias: float32 [1024], replicated
- w_qkv: bfloat16 [3, 1024, 16, 64], P(None, None, 'tp')
- b_qkv: float32 [3, 16, 64], P(None, 'tp')
- w_out: bfloat16 [16, 64, 1024], P('tp')
- b_out: float32 [1024], replicated
- ln2_gain: float32 [1024], replicated
- ln2_bias: float32 [1024], replicated
- w_up: bfloat16 [1024, 4096], P(None, 'tp')
- b_up: float32 [4096], P('tp')
- w_down: bfloat16 [4096, 1024], P('tp')
- b_down: float32 [1024], replicated
Outputs:
- output 1: bfloat16 [32, 512, 1024], P('dp', 'tp'), parts along dimension 0
- output 2: bfloat16 [32, 512, 1024], P('dp', 'tp'), parts along dimension 0
- output 3: float32 [2048], P('dp'), parts along dimension 0
- output 4: float32 [2048], P('dp'), parts along dimension 0
- output 5: float32 [6, 1024, 16, 64], P('dp', None, 'tp'), parts along dimension 0
- output 6: float32 [6, 16, 64], P('dp', 'tp'), parts along dimension 0
- output 7: float32 [32, 64, 1024], P(('dp', 'tp')), parts along dimension 0
- output 8: float32 [2048], P('dp'), parts along dimension 0
- output 9: float32 [2048], P('dp'), parts along dimension 0
- output 10: float32 [2048], P('dp'), parts along dimension 0
- output 11: float32 [2048, 4096], P('dp', 'tp'), parts along dimension 0
- output 12: float32 [8192], P(('dp', 'tp')), parts along dimension 0
- output 13: float32 [8192, 1024], P(('dp', 'tp')), parts along dimension 0
- output 14: float32 [2048], P('dp'), parts along dimension 0
There are 2 independent parts. A program takes and returns all parts, laid end to end along the dimension named above; an argument that names none is the same for every part.
All inputs are finite; a program needn't handle non-finite values.
Results may differ from a plain program's by a relative error of at most 0.0122089.
Values are sent between devices in bfloat16 or wider.
A program may use at most 768 MiB of HBM per device.

v0:
```python
import functools

import jax
import jax.numpy as jnp
import numpy as np
from jax import lax
from jax.experimental import pallas as pl
from jax.experimental.pallas import tpu as pltpu
from jax.sharding import PartitionSpec as P

LN_EPS = 1e-5
ROPE_BASE = 10000.0
INV_SQRT2 = 0.7071067811865476
INV_SQRT_2PI = 0.3989422804014327
NEG_LARGE = -1e30
F32 = jnp.float32
BF16 = jnp.bfloat16
VMEM_LIMIT = 66_500_000
LANES = 128
NN = (((1,), (0,)), ((), ()))
NT = (((1,), (1,)), ((), ()))
TN = (((0,), (0,)), ((), ()))
PAIR, FAR, CROSS = 1, 2, 3
FAR0 = FAR + FAR
FAR1 = FAR0 + 1
BOTH = range(2)
ANY = pl.BlockSpec(memory_space=pl.ANY)


def mm(a, b, dims):
    return lax.dot_general(a, b, dims, preferred_element_type=F32)


def ln_stats(v):
    centered = v - jnp.mean(v, axis=-1, keepdims=True)
    inv_std = lax.rsqrt(jnp.mean(centered * centered, axis=-1, keepdims=True) + LN_EPS)
    return centered * inv_std, inv_std


def ln_grad(d_out, x_hat, inv_std, gain):
    d_hat = d_out * gain
    return inv_std * (d_hat - jnp.mean(d_hat, axis=-1, keepdims=True) - x_hat * jnp.mean(d_hat * x_hat, axis=-1, keepdims=True))


def col_sum(t):
    return jnp.sum(t, axis=0, keepdims=True)


def swap_halves(t, head_dim):
    half = head_dim // 2
    lane = lax.broadcasted_iota(jnp.int32, t.shape, t.ndim - 1)
    return jnp.where(lane % head_dim < half, pltpu.roll(t, t.shape[-1] - half, t.ndim - 1), pltpu.roll(t, half, t.ndim - 1))


def span(i, n):
    return pl.ds(pl.multiple_of(i * n, n), n)


def fold(row, out, first):
    for i in range(row.shape[-1] // LANES):
        out[pl.ds(first + i, 1), :] = row[:, i * LANES:(i + 1) * LANES]


def unfold(src, first, out):
    for i in range(out.shape[-1] // LANES):
        out[:, pl.ds(i * LANES, LANES)] = src[pl.ds(first + i, 1), :]


def loop_rows(total, n, body):
    @pl.loop(0, total // n)
    def _(i):
        body(span(i, n))


class Net:
    def __init__(self, n_tp, send, recv, local):
        self.n_tp, self.send, self.recv, self.local = n_tp, send, recv, local
        self.copies, self.count, self.n_local = {}, 0, 0

    def peer(self, chip, core=0):
        me = lax.axis_index('tp')
        way = 1 - 2 * lax.rem(lax.div(me, 2), 2)
        at = lax.rem(me + 2 * chip * way + self.n_tp, self.n_tp) if chip else me
        return at + 1 - 2 * lax.rem(at, 2) if core else at

    def add(self, name, src, dst, chip, core=0):
        n = self.count
        self.count += 1

        def make():
            return pltpu.make_async_remote_copy(
                src_ref=src(), dst_ref=dst(), send_sem=self.send.at[n], recv_sem=self.recv.at[n],
                device_id={'tp': self.peer(chip, core)}, device_id_type=pl.DeviceIdType.MESH)

        self.copies.setdefault(name, []).append(make)

    def add_local(self, name, src, dst):
        n = self.n_local
        self.n_local += 1
        self.copies.setdefault(name, []).append(lambda: pltpu.make_async_copy(src(), dst(), self.local.at[n]))

    def start(self, *names):
        for name in names:
            for make in self.copies[name]:
                make().start()

    def got(self, *names):
        for name in names:
            with jax.named_scope('got_' + name):
                for make in self.copies[name]:
                    make().wait_recv()

    def sent(self, *names):
        for name in names:
            for make in self.copies[name]:
                make().wait_send()

    def done(self, *names):
        for name in names:
            with jax.named_scope('done_' + name):
                for make in self.copies[name]:
                    make().wait()

    def gather(self, name, own, buf):
        for stage, chip in (('p', PAIR), ('c', CROSS)):
            self.add(name + stage, lambda: own, lambda c=chip: buf.at[2 * c], chip)
        self.add(name + 'm', lambda: own, lambda: buf.at[1], 0, 1)
        for stage, chip in (('f', PAIR), ('g', CROSS)):
            self.add(name + stage, lambda c=chip: buf.at[2 * c], lambda c=chip: buf.at[2 * c + 1], 0, 1)

    def gather_far(self, name, src, here, other, via):
        self.add(name + 'r', src, here, via)
        self.add(name + 'l', here, other, 0, 1)

    def exchange(self, name, src, dst, rows):
        me = lax.axis_index('tp')
        for core in BOTH:
            for chip in (PAIR, CROSS, FAR, 0):
                if chip + core:
                    self.add(name, lambda c=chip, k=core: src.at[span(self.peer(c, k), rows)], lambda: dst.at[span(me, rows)], chip, core)
        self.add_local(name + '_own', lambda: src.at[span(me, rows)], lambda: dst.at[span(me, rows)])

    def multicast(self, name, src, dst, pair_dst, rows):
        me = lax.axis_index('tp')
        at = lambda buf: (lambda: buf.at[span(me, rows)])
        other = {0: PAIR, PAIR: 0, CROSS: FAR}
        for chip, stage in ((CROSS, '_cross'), (PAIR, '_pair'), (0, '_pair')):
            for core in BOTH:
                if chip + core:
                    for c, buf in ((chip, dst), (other[chip], pair_dst)):
                        self.add(name + stage, lambda c=c, k=core: src.at[span(self.peer(c, k), rows)], at(buf), chip, core)
        for c, buf in ((0, dst), (PAIR, pair_dst)):
            self.add_local(name + '_own', lambda c=c: src.at[span(self.peer(c), rows)], at(buf))
        came = lambda buf: (lambda: buf.at[span(lax.div(self.peer(CROSS), 2), 2 * rows)])
        self.add(name + '_fwd', came(dst), came(pair_dst), PAIR)
        self.add(name + '_fwd', came(pair_dst), came(dst), PAIR)


def solution(mesh):
    n_tp = mesh.shape['tp']
    n_chips = n_tp // 2
    act_spec = P('dp', 'tp', None)
    rep_vec = P(None)
    part_vec = P('dp')
    in_specs = (act_spec, act_spec, P('dp', None), rep_vec, rep_vec, P(None, None, 'tp', None), P(None, 'tp', None),
                P('tp', None, None), rep_vec, rep_vec, rep_vec, P(None, 'tp'), P('tp'), P('tp', None), rep_vec)
    out_specs = (act_spec, act_spec, part_vec, part_vec, P('dp', None, 'tp', None), P('dp', 'tp', None),
                 P(('dp', 'tp'), None, None), part_vec, part_vec, part_vec, P('dp', 'tp'), P(('dp', 'tp')),
                 P(('dp', 'tp'), None), part_vec)

    def device_step(x_in, grad_y, pad_mask, ln1_gain, ln1_bias, w_qkv, b_qkv, w_out, b_out, ln2_gain, ln2_bias, w_up, b_up, w_down, b_down):
        batch, p_len, dim = x_in.shape
        seq = pad_mask.shape[1]
        _, _, heads, hd = w_qkv.shape
        seqs = batch // n_tp
        ffn = w_up.shape[1]
        width = heads * hd
        n3 = 3 * width
        tok = seqs * seq
        chunk = seqs * p_len
        qc = seq // 2
        q_scale = hd ** -0.5
        sds = jax.ShapeDtypeStruct
        n_tile = n3 + width
        half = dim // 2
        twice = n_tp + n_tp
        quarter = ffn // 2
        v_half = 3 * n_tp

        def kernel(*refs):
            it = iter(refs)
            take = lambda n: [next(it) for _ in range(n)]
            (x_ref, dy_ref, wq_ref, bq_ref, wo_ref, wu_ref, bu_ref, wd_ref), plain = take(8), take(8)
            y_out, gx_out, g_up, g_down, g_q, g_o, g_vec, g_b, wq, wu, wd, q_hbm, k_hbm, v_hbm, act_hbm, slope_hbm = take(16)
            p_at, got_at, sum_at, early_at, last_at, x_dn, x_up, p_dn, p_up, r_dn, r_up = take(11)
            x, h1, dy, x1, h2, dx1b, h2p, dyp, y, o4, do4, wo, acc, acc2, p_rcv, p_snd, d4 = take(17)
            dq_acc, dk_acc, dv_acc, cos_t, sin_t, ok, m_st, l_st, b_att, b_ffn, u_all, gb, b_all, b8, late, late_in, vec, mate, mate_in, v_own = take(20)
            dpre = next(it)
            act_p, dpre_p = (y.at[:, pl.ds(i * ffn, ffn)] for i in BOTH)
            here = take(8)
            send, recv, local, pair_send, pair_recv, pair_ready = take(6)
            net = Net(n_tp, send, recv, local)
            me = lax.axis_index('tp')
            mask_ref, gain1, bias1, bias_o, gain2, bias_d, bias2, freq_ref = here

            net.gather('q', wq_ref, wq)
            net.gather('o', wo_ref, wo)
            net.gather('u', wu_ref, wu)
            net.gather('d', wd_ref, wd)
            for name, buf in (('q', wq), ('o', wo), ('u', wu)):
                net.gather_far(name, lambda b=buf: b.at[2 * PAIR], lambda b=buf: b.at[FAR0], lambda b=buf: b.at[FAR1], CROSS)
            for i in BOTH:
                mine = lambda core, i=i: dx1b.at[pl.ds(core * ffn + i * quarter, quarter)]
                net.gather_far(f'd{i}', lambda i=i: wd.at[2 * CROSS, pl.ds(i * quarter, quarter)], lambda m=mine: m(0), lambda m=mine: m(1), PAIR)
            net.exchange('x', x_ref, x, chunk)
            net.multicast('dy', dy_ref, dy, dyp, chunk)
            net.exchange('y', y, y_out, chunk)
            net.exchange('gx', h1, gx_out, chunk)
            for chip in range(n_chips):
                for core in BOTH:
                    if chip + core:
                        slot = 2 * chip + core
                        net.add('bias', lambda: bq_ref, lambda n=slot: b_all.at[n], chip, core)
                        net.add('bias', lambda: bu_ref, lambda n=slot: u_all.at[n], chip, core)
            for chip in (PAIR, CROSS, FAR):
                net.add('late', lambda n=chip: late.at[n], lambda n=chip: late_in.at[n], chip)
            side = lax.rem(me, 2)
            net.add('mate', lambda: mate, lambda: mate_in, 0, 1)
            net.add('final', lambda: v_own.at[span(side, v_half)], lambda: v_own.at[span(side, v_half)], 0, 1)
            for i in BOTH:
                net.add(f'h{i}', lambda p=pl.ds(i * half, half): h2.at[p], lambda p=pl.ds(i * half, half): h2p.at[p], PAIR)
            net.add('dn_x', lambda: x_dn, lambda: r_dn, CROSS)
            net.add('up_x', lambda: x_up, lambda: r_up, CROSS)
            net.add('at_early', lambda: p_at.at[PAIR], lambda: early_at, PAIR)
            t_half = n_tile // 2
            for i, part in enumerate((pl.ds(0, t_half), pl.ds(t_half, t_half))):
                net.add(f'at_relay{i}', lambda p=part: p_at.at[FAR, p], lambda p=part: got_at.at[p], PAIR)
                net.add(f'at_sum{i}', lambda p=part: sum_at.at[p], lambda p=part: last_at.at[p], CROSS)
                net.add_local(f'at{i}_load', lambda p=part: got_at.at[p], lambda p=part: p_rcv.at[0, p])
                net.add_local(f'at{i}_load', lambda p=part: p_at.at[CROSS, p], lambda p=part: p_rcv.at[1, p])
                net.add_local(f'at{i}_store', lambda p=part: p_rcv.at[1, p], lambda p=part: sum_at.at[p])
            for src, dst in zip(plain, here):
                net.add_local('own', lambda r=src: r, lambda r=dst: r)
            net.add_local('write', lambda: v_own, lambda: g_vec)
            net.add_local('write', lambda: b8.at[0], lambda: g_b)
            for ref, tmp, buf in ((wq_ref, lambda: h2.at[pl.ds(0, n3)], wq), (wu_ref, lambda: x1.at[:, pl.ds(0, ffn)], wu),
                                        (wd_ref, lambda: dx1b.at[pl.ds(0, ffn)], wd)):
                net.add_local('load', lambda r=ref: r, tmp)
                net.add_local('store', tmp, lambda b=buf: b.at[0])
            net.add_local('own', lambda: wo_ref, lambda: wo.at[0])
            net.add_local('own', lambda: bq_ref, lambda: b_all.at[0])
            net.add_local('own', lambda: bu_ref, lambda: u_all.at[0])
            def pass_on(i, stage):
                if stage == 0:
                    net.got(f'at_relay{i}')
                    net.start(f'at{i}_load')
                elif stage == 1:
                    net.done(f'at{i}_load')

                    def body(rows):
                        rows = pl.ds(i * t_half + rows.start, rows.size)
                        p_rcv[1, rows] += p_rcv[0, rows]

                    loop_rows(t_half, 8, body)
                    net.start(f'at{i}_store')
                else:
                    net.done(f'at{i}_store')
                    net.start(f'at_sum{i}')

            def hooks(step, table):
                for at, act in table.items():
                    @pl.when(step == at)
                    def _(act=act):
                        act()

            tile_order = (FAR, PAIR, CROSS, 0)

            def place(i):
                return jnp.where(i == 0, FAR, jnp.where(i == 1, PAIR, jnp.where(i == 2, CROSS, 0)))

            def order(s):
                return 2 * place(lax.div(s, 2)) + 1 - lax.rem(s, 2)

            def to_partner(src, dst, sem):
                return pltpu.make_async_remote_copy(
                    src_ref=p_snd.at[src], dst_ref=p_rcv.at[dst], send_sem=pair_send.at[sem], recv_sem=pair_recv.at[sem],
                    device_id={'tp': net.peer(0, 1)}, device_id_type=pl.DeviceIdType.MESH)

            def keep(i, to):
                return pltpu.make_async_copy(p_rcv.at[i], to, pair_send.at[twice + i])

            def into(i):
                return lambda at, v: p_snd.__setitem__((i,) + at, v)

            def add_sent(i, j):
                def body(rows):
                    p_rcv[j, rows] += p_snd[i, rows]

                loop_rows(n_tile, 16, body)

            def pair_go(s):
                @pl.when(lax.rem(s, 2) == 1)
                def _():
                    to_partner(0, lax.div(s, 2), lax.div(s, 2)).start()

            def pair(s, tile):
                j = lax.div(s, 2)
                odd = lax.rem(s, 2)
                tile(into(odd))

                @pl.when(odd == 1)
                def _():
                    copy = to_partner(0, j, j)
                    copy.wait_send()
                    copy.wait_recv()
                    add_sent(1, j)
                    keep(j, p_at.at[place(j)]).start()

            def stored(i):
                keep(i, p_at.at[tile_order[i]]).wait()

            def pair_begin():
                pl.semaphore_signal(pair_ready, inc=1, device_id={'tp': net.peer(0, 1)}, device_id_type=pl.DeviceIdType.MESH)
                pl.semaphore_wait(pair_ready, 1)

            barrier = pltpu.get_barrier_semaphore()
            for chip in range(n_chips):
                for core in BOTH:
                    if chip + core:
                        pl.semaphore_signal(barrier, inc=1, device_id={'tp': net.peer(chip, core)}, device_id_type=pl.DeviceIdType.MESH)
            pl.semaphore_wait(barrier, n_tp - 1)
            net.start('qp', 'qc', 'x', 'qm', 'bias', 'own', 'load', 'x_own', 'dy_own')
            net.done('own')
            angle = lax.broadcasted_iota(jnp.int32, (seq, width), 0).astype(F32) * freq_ref[0:1, :]
            cos_t[...] = jnp.cos(angle)
            sin_t[...] = jnp.sin(angle) * freq_ref[1:2, :]
            for b in range(seqs):
                row = mask_ref[pl.ds(me * seqs + b, 1), :].astype(F32)
                ok[b] = jnp.broadcast_to(row, (LANES, seq)).T
            net.done('load')
            net.start('store')
            net.got('qp', 'qc')
            net.start('qr', 'dy_cross', 'oc', 'op', 'up', 'dy_pair', 'qf', 'qg', 'om')
            net.done('x_own', 'dy_own')
            net.got('bias')
            for n in range(n_tp):
                b = b_all[n]
                b_att[n] = jnp.concatenate([b[i // heads, i % heads:i % heads + 1, :] for i in range(3 * heads)], axis=1)
                b_ffn[n] = u_all[n]
            net.got('x')

            def ln1(rows):
                x_hat, _ = ln_stats(x[rows, :].astype(F32))
                h1[rows, :] = (x_hat * gain1[...] + bias1[...]).astype(BF16)

            loop_rows(tok, chunk, ln1)
            net.done('store')
            net.got('qm', 'qf', 'qg')

            def arrival(s):
                return s + 2 * lax.div(s, n_chips) - n_chips * lax.div(s, n_chips + 2)

            def qkv_step(ps, w, q_ref, k_ref, v_ref):
                s = ps.index[0]
                hooks(s, {2: lambda: (net.got('op'), net.start('or', 'uc', 'um', 'of')), 4: lambda: (net.got('qr'), net.start('ql')),
                          5: lambda: net.got('ql')})
                n_src = tok // chunk // 2

                @pl.loop(0, 2)
                def _(i):
                    rows = span(i, tok // 2)
                    t = mm(h1[rows, :], w[0], NT) + b_att[arrival(s)]
                    cos, sin = (t_ref[span(i, seq // 2), :].reshape(n_src, 1, p_len, width) for t_ref in (cos_t, sin_t))

                    def rope(v):
                        out = v.reshape(n_src, seqs, p_len, width) * cos + swap_halves(v, hd).reshape(n_src, seqs, p_len, width) * sin
                        return out.astype(BF16)

                    src = span(i, n_src)
                    q_ref[0, src] = rope(t[:, :width] * q_scale)
                    k_ref[0, src] = rope(t[:, width:2 * width])
                    v_ref[0, src] = t[:, 2 * width:].reshape(n_src, seqs, p_len, width).astype(BF16)

            slot3 = lambda rows, cols, f=lambda s: s: pl.BlockSpec((1, rows, cols), lambda s: (f(s), 0, 0))

            def pipe(body, **specs):
                def run(*refs):
                    with jax.named_scope(body.__name__):
                        pltpu.emit_pipeline(body, _explicit_indices=True, **specs)(*refs)

                return run

            pipe(qkv_step, grid=(n_tp,), in_specs=[slot3(n3, dim, arrival)],
                 out_specs=[pl.BlockSpec((1, n_tp, seqs, p_len, width), lambda s: (arrival(s), 0, 0, 0, 0))] * 3)(
                wq, q_hbm, k_hbm, v_hbm)

            srcs = qc // p_len
            lane = lax.broadcasted_iota(jnp.int32, (qc, width), 1)

            def attn_step(ps, q_ref, k_ref, v_ref):
                g, b = ps.index
                hooks(g * seqs + b, {
                    8: lambda: (net.got('dy_cross'), net.start('dy_fwd')), 9: lambda: (net.got('up'), net.start('ur', 'dc', 'dm', 'uf')),
                    14: lambda: (net.got('oc', 'or'), net.start('og', 'ol'))})
                bad = ok[b][:, 0:1] <= 0
                k = k_ref[0, :, 0].reshape(seq, width)
                v_t = v_ref[0, :, 0].reshape(seq, width).T
                for c in range(seq // qc):
                    src = slice(c * srcs, (c + 1) * srcs)
                    cols = slice(c * qc, (c + 1) * qc)
                    q = q_ref[0, src, 0].reshape(qc, width)
                    outs = []
                    for h in range(heads):
                        s = jnp.where(bad, NEG_LARGE, mm(k, jnp.where(lane // hd == h, q, jnp.zeros_like(q)), NT))
                        m = jnp.max(s, axis=0, keepdims=True)
                        e = jnp.exp(s - m)
                        r = 1.0 / col_sum(e)
                        outs.append(mm(v_t[h * hd:(h + 1) * hd], (e * r).astype(BF16), NN))
                        m_st[g, b, h:h + 1, cols] = m
                        l_st[g, b, h:h + 1, cols] = r
                    o4[src, b, :, span(g, width)] = jnp.concatenate(outs, axis=0).T.astype(BF16).reshape(srcs, p_len, width)

            head_blk = pl.BlockSpec((1, n_tp, 1, p_len, width), lambda g, b: (g, 0, b, 0, 0))
            pipe(attn_step, grid=(n_tp, seqs), in_specs=[head_blk] * 3)(q_hbm, k_hbm, v_hbm)

            net.got('om', 'of', 'og', 'ol')

            @pl.loop(0, tok // (2 * chunk))
            def _(i):
                rows = span(i, 2 * chunk)
                o = o4[pl.ds(2 * i, 2)].reshape(2 * chunk, n_tp * width)
                low = (x[rows, :].astype(F32) + (mm(o, wo[...].reshape(n_tp * width, dim), NN) + bias_o[...])).astype(BF16)
                x1[rows, :] = low
                x_hat, _ = ln_stats(low.astype(F32))
                h2[rows, :] = (x_hat * gain2[...] + bias2[...]).astype(BF16)

            net.start('h0', 'h1', 'dp')

            def gelu(pre):
                erf_term = lax.erf(pre * INV_SQRT2)
                act = (0.5 * pre * (1.0 + erf_term)).astype(BF16)
                return act, 0.5 * (1.0 + erf_term) + pre * jnp.exp(-0.5 * pre * pre) * INV_SQRT_2PI

            cols = lambda f: pl.BlockSpec((tok, ffn), lambda s: (0, f(s)))
            wu_spec, wd_spec = functools.partial(slot3, dim, ffn), functools.partial(slot3, ffn, dim)

            def mlp_up(n, f, table):
                def up_step(ps, w, act_ref, slope_ref):
                    s = ps.index[0]
                    hooks(s, table)

                    def body(rows):
                        act_ref[rows, :], slope_ref[rows, :] = gelu(mm(h2[rows, :], w[0], NN) + b_ffn[f(s)])

                    loop_rows(tok, half, body)

                pipe(up_step, grid=(n,), in_specs=[wu_spec(f)], out_specs=[cols(f)] * 2)(wu, act_hbm, slope_hbm)

            net.got('um', 'uf')
            mlp_up(n_tp - 2, arrival, {2: lambda: (net.got('uc'), net.start('ug')), 3: lambda: net.got('ug')})
            net.got('dy_pair', 'dy_fwd', 'dm')

            def backward(slot, w_d, w_u, act_ref, slope_ref, add):
                if add:
                    gb[slot] = jnp.zeros_like(gb[0])

                def body(rows):
                    d_pre = mm(dy[rows, :], w_d, NT) * slope_ref[rows, :]
                    low = d_pre.astype(BF16)
                    dpre[rows, :] = low
                    if add:
                        gb[slot] += col_sum(d_pre)
                        acc[rows, :] += mm(act_ref[rows, :], w_d, NN)
                        acc2[rows, :] += mm(low, w_u, NT)

                loop_rows(tok, half, body)

            def pair_gelu(rows, w_u, slot):
                return gelu(mm(h2p[rows, :], w_u, NN) + b_ffn[slot])

            def grads(chip, at, x_ref, between):
                f = lambda s: 2 * chip + 1 - s
                copy = to_partner(0, at, n_tp + at)

                def first(ps, w_u, act_ref):
                    s = ps.index[0]
                    rows = pl.ds(0, half)
                    act_p[rows, :] = pair_gelu(rows, w_u[0], f(s))[0]
                    p_snd[s] = mm(act_ref[...], dy[...], TN) + mm(act_p[rows, :], dyp[rows, :], TN)

                def second(ps, w_u):
                    s = ps.index[0]
                    pl.when(s == 1)(lambda: copy.start())
                    rows = pl.ds(half, half)
                    act_p[rows, :] = pair_gelu(rows, w_u[0], f(s))[0]
                    p_snd[s] += mm(act_p[rows, :], dyp[rows, :], TN)

                    @pl.when(s == 1)
                    def _():
                        copy.wait_recv()
                        add_sent(1, at)
                        keep(at, x_ref).start()
                        copy.wait_send()

                pipe(first, grid=(len(BOTH),), in_specs=[wu_spec(f), cols(f)])(wu, act_hbm)
                between()
                pipe(second, grid=(len(BOTH),), in_specs=[wu_spec(f)])(wu)
                keep(at, x_ref).wait()

            def mlp(n, f, add, table, last=None):
                def mlp_step(ps, wd_s, wu_s, act_ref, slope_ref):
                    s = ps.index[0]
                    backward(f(s), wd_s[0], wu_s[0], act_ref, slope_ref, add)
                    if last:
                        at, ref, send = last
                        copy = to_partner(0, at + 1, n_tp + at + 1)
                        pl.when(s == 1)(lambda: copy.start())

                        @pl.when(s < 2)
                        def _():
                            def body(rows):
                                dpre_p[rows, :] = (mm(dyp[rows, :], wd_s[0], NT) * pair_gelu(rows, wu_s[0], f(s))[1]).astype(BF16)

                            loop_rows(tok, half, body)
                            for i in BOTH:
                                part = pl.ds(i * half, half)
                                p_snd[s, pl.ds(0, ffn), part] = mm(h2[:, part], dpre[...], TN) + mm(h2p[:, part], dpre_p[...], TN)

                        @pl.when(s == 1)
                        def _():
                            copy.wait_recv()
                            add_sent(1, at + 1)
                            keep(at + 1, ref).start()
                            copy.wait_send()

                    hooks(s, table)

                pipe(mlp_step, grid=(n,), in_specs=[wd_spec(f), wu_spec(f), cols(f), cols(f)])(wd, wu, act_hbm, slope_hbm)

            acc[...] = jnp.zeros_like(acc)
            acc2[...] = jnp.zeros_like(acc2)
            mlp(2, lambda s: s, True, {})
            net.got('ur')
            net.start('ul')
            net.got('ul')
            mlp_up(2, lambda s: s + FAR0, {})
            net.got('h0')
            grads(CROSS, 0, x_dn, lambda: (net.got('dc'), net.start('dg', 'd0r', 'd1r'), net.got('h1')))
            net.start('dn_x')
            net.got('dg')

            def sent_up():
                keep(1, x_up).wait()
                net.start('up_x')

            slots = lambda s: jnp.where(s < 2, 2 * CROSS + 1 - s, s)
            mlp(n_chips, slots, True, {0: lambda: (net.got('dp'), net.start('df')), 1: lambda: net.got('df'), 2: sent_up}, (0, x_up, 'up_x'))

            for slot in (FAR0, FAR1):
                gb[slot] = jnp.zeros_like(gb[slot])

            def far_step(ps, w_u, act_ref, slope_ref):
                part, core = ps.index
                hooks(2 * part + core, {0: lambda: (net.got('d0r'), net.start('d0l')), 1: lambda: net.got('d0l'),
                                        2: lambda: (net.got('d1r'), net.start('d1l')), 3: lambda: net.got('d1l')})
                w_d = dx1b[pl.ds(pl.multiple_of(core * ffn + part * quarter, quarter), quarter), :]

                def body(rows):
                    d_pre = mm(dy[rows, :], w_d, NT) * slope_ref[rows, :]
                    gb[FAR0 + core, :, span(part, quarter)] += col_sum(d_pre)
                    acc[rows, :] += mm(act_ref[rows, :], w_d, NN)
                    acc2[rows, :] += mm(d_pre.astype(BF16), w_u[0], NT)

                loop_rows(tok, half, body)

            narrow = pl.BlockSpec((tok, quarter), lambda part, core: (0, 2 * (FAR0 + core) + part))
            pipe(far_step, grid=(len(BOTH),) * len(BOTH), in_specs=[pl.BlockSpec((1, dim, quarter), lambda part, core: (FAR0 + core, 0, part)), narrow, narrow])(
                wu, act_hbm, slope_hbm)

            def y_rows(rows):
                y[rows, :] = (x1[rows, :].astype(F32) + (acc[rows, :] + bias_d[...])).astype(BF16)

            loop_rows(tok, 2 * chunk, y_rows)
            vec[...] = jnp.zeros_like(vec)
            net.start('y', 'y_own')
            net.sent('d0l', 'd1l')

            @pl.loop(0, tok // (2 * chunk))
            def _(i):
                rows = span(i, 2 * chunk)
                x1_f, dy_f, dh = x1[rows, :].astype(F32), dy[rows, :].astype(F32), acc2[rows, :]
                x_hat, inv_std = ln_stats(x1_f)
                d_x1 = dy_f + ln_grad(dh, x_hat, inv_std, gain2[...])
                acc2[rows, :] = d_x1
                low = d_x1.astype(BF16)
                dx1b[rows, :] = low
                d_o = mm(low, wo[...].reshape(n_tp * width, dim), NT).astype(BF16)
                do4[pl.ds(2 * i, 2)] = d_o.reshape(2, seqs, p_len, n_tp * width)
                for n, t in enumerate((d_x1, dh * x_hat, dh, dy_f)):
                    vec[2 + n:3 + n, :] += col_sum(t)

            pair_begin()

            def bwd_step(ps, q_ref, k_ref, v_ref, w):
                step = ps.index[0]
                g = order(step)
                hooks(step, {2: lambda: (stored(0), net.start('at_relay0', 'at_relay1')),
                             4: lambda: (stored(1), net.start('at_early')), 6: lambda: (stored(2), pass_on(0, 0)), 7: lambda: pass_on(0, 2)})
                pair_go(step)
                b8[g] = jnp.zeros_like(b8[0])
                fold(gb[g], b8.at[g], 3)
                for b in range(seqs):
                    bad = ok[b][:, 0:1] <= 0
                    k = k_ref[0, :, b].reshape(seq, width)
                    v = v_ref[0, :, b].reshape(seq, width)
                    k_t = k.T
                    for c in range(seq // qc):
                        src = slice(c * srcs, (c + 1) * srcs)
                        at = slice(c * qc, (c + 1) * qc)
                        q = q_ref[0, src, b].reshape(qc, width)
                        d_o = do4[src, b, :, span(g, width)].reshape(qc, width)
                        dk = jnp.zeros((seq, width), F32)
                        dv = jnp.zeros((seq, width), F32)
                        dqs = []
                        for h in range(heads):
                            mine = lane // hd == h
                            q_h = jnp.where(mine, q, jnp.zeros_like(q))
                            do_h = jnp.where(mine, d_o, jnp.zeros_like(d_o))
                            s = jnp.where(bad, NEG_LARGE, mm(k, q_h, NT))
                            p = jnp.exp(s - m_st[g, b, h:h + 1, at]) * l_st[g, b, h:h + 1, at]
                            dv += mm(p.astype(BF16), do_h, NN)
                            dp = mm(v, do_h, NT)
                            ds = (p * (dp - col_sum(dp * p))).astype(BF16)
                            dk += mm(ds, q_h, NN)
                            dqs.append(mm(k_t[h * hd:(h + 1) * hd], ds, NN))
                        dq_acc[at, :] = jnp.concatenate(dqs, axis=0).T
                        dk_acc[...] = dk if c == 0 else dk_acc[...] + dk
                        dv_acc[...] = dv if c == 0 else dv_acc[...] + dv
                    cos, sin = cos_t[...], sin_t[...]
                    dq, dk, dv = dq_acc[...], dk_acc[...], dv_acc[...]
                    dq = (dq * cos - swap_halves(dq, hd) * sin) * q_scale
                    dk = dk * cos - swap_halves(dk, hd) * sin
                    for i, t in enumerate((dq, dk, dv)):
                        d4[:, b, :, i * width:(i + 1) * width] = t.astype(BF16).reshape(n_tp, p_len, width)
                        b8[g, i:i + 1, :] += col_sum(t)

                @pl.when(step == 0)
                def _():
                    acc[...] = jnp.zeros_like(acc)

                @pl.loop(0, 2)
                def _(i):
                    acc[span(i, half), :] += mm(d4[pl.ds(n_chips * i, n_chips)].reshape(half, n3), w[0], NN)

                def tile(put):
                    put((pl.ds(0, n3),), mm(d4[...].reshape(tok, n3), h1[...], TN))
                    put((pl.ds(n3, width),), mm(o4[:, :, :, span(g, width)].reshape(tok, width), dx1b[...], TN))

                pair(step, tile)
                hooks(step, {6: lambda: pass_on(0, 1)})

            slot_blk = pl.BlockSpec((1, n_tp, seqs, p_len, width), lambda s: (order(s), 0, 0, 0, 0))
            pipe(bwd_step, grid=(n_tp,), in_specs=[slot_blk] * 3 + [slot3(n3, dim, order)])(
                q_hbm, k_hbm, v_hbm, wq)

            pass_on(1, 0)

            def ln1_bwd(rows):
                x_hat, inv_std = ln_stats(x[rows, :].astype(F32))
                dh = acc[rows, :]
                h1[rows, :] = (acc2[rows, :] + ln_grad(dh, x_hat, inv_std, gain1[...])).astype(BF16)
                vec[0:1, :] += col_sum(dh * x_hat)
                vec[1:2, :] += col_sum(dh)

            loop_rows(tok, 2 * chunk, ln1_bwd)
            stored(3)
            for r in range(6):
                fold(vec[pl.ds(r, 1), :], v_own, r * n_tp)
            mate[0:v_half] = v_own[span(1 - side, v_half), :]
            for n in range(n_chips):
                mate[pl.ds(v_half + n * 8, 8)] = b8[2 * n + 1]
            net.start('mate')
            pass_on(1, 1)
            net.got('mate')
            v_sum = v_own[span(side, v_half), :] + mate_in[0:v_half]
            for n in range(n_chips):
                late[n, 0:v_half] = v_sum
                late[n, v_half:] = b8[2 * n] + mate_in[pl.ds(v_half + n * 8, 8)]
            net.start('late')
            pass_on(1, 2)
            net.start('gx', 'gx_own')

            net.sent('y')
            net.done('y_own')
            pair_begin()
            grads(0, 2, p_dn, lambda: None)
            mlp(2, lambda s: 1 - s, False, {}, (2, p_up, None))
            keep(3, p_up).wait()

            def total(refs, out, block, at):
                def body(*blocks):
                    v = blocks[1][...]
                    for more in blocks[2:-1]:
                        v += more[...]
                    blocks[-1][...] = v

                pipe(body, grid=(len(BOTH),), in_specs=[pl.BlockSpec(block, at)] * len(refs),
                     out_specs=[pl.BlockSpec(block, lambda i: (i, 0))])(*refs, out)

            by_row, by_col = lambda i: (i, 0), lambda i: (0, i)
            net.got('late')
            late_sum = late[0]
            for n in range(1, n_chips):
                late_sum += late_in[n]
            v_own[span(side, v_half), :] = late_sum[0:v_half]
            b8[0] = late_sum[v_half:]
            net.start('final')
            net.got('dn_x', 'up_x')
            total((p_dn, r_dn), g_down, (t_half, dim), by_row)
            total((p_up, r_up), g_up, (n_tile, half), by_col)
            net.got('at_early', 'at_sum0', 'at_sum1')
            for rows, out, n in ((pl.ds(0, n3), g_q, n3), (pl.ds(n3, width), g_o, width)):
                total((p_at.at[0, rows], early_at.at[rows], last_at.at[rows]), out, (n // 2, dim), by_row)
            for name in net.copies:
                if name not in ('load', 'store', 'own', 'write', 'gx', 'y', 'd0l', 'd1l') and not name.endswith(('_own', '_load', '_store')):
                    net.sent(name)
            net.got('y', 'final')
            net.start('write')
            net.done('gx_own', 'write')
            net.got('gx')
            net.sent('gx')

        big = (tok, dim)
        shapes = lambda *dims, dtype=F32: sds(dims, dtype)
        flat = lambda t: t.reshape(tok, dim)
        inv_freq = ROPE_BASE ** (-2.0 * np.arange(hd // 2) / hd)
        sign = np.repeat([-1.0, 1.0], hd // 2)
        freq = np.stack([np.tile(inv_freq, 2 * heads), np.tile(sign, heads)]).astype(np.float32)
        line = lambda v: v.reshape(1, -1)
        sem = lambda n: pltpu.SemaphoreType.DMA((n,))
        low = functools.partial(shapes, dtype=BF16)
        weights = [low(n_tp, n3, dim), low(n_tp, dim, ffn), low(n_tp, ffn, dim)]
        tiles = [shapes(n_chips, n_tile, dim)] + [shapes(n_tile, dim)] * 10
        out_shape = ([low(*big)] * 2 + [shapes(dim, ffn), shapes(ffn, dim), shapes(n3, dim), shapes(width, dim), shapes(6 * n_tp, LANES), shapes(8, LANES)] + weights
                     + [low(n_tp, n_tp, seqs, p_len, width)] * 3 + [low(tok, n_tp * ffn), shapes(tok, n_tp * ffn)] + tiles)
        plain = [pad_mask] + [line(v) for v in (ln1_gain, ln1_bias, b_out, ln2_gain, b_down, ln2_bias)] + [freq]
        heads4 = low(n_tp, seqs, p_len, n_tp * width)
        stat = shapes(n_tp, seqs, heads, seq)
        tile8 = shapes(n_tp, 8, LANES)
        late = shapes(n_chips, v_half + 8, LANES)
        mate = shapes(v_half + 8 * n_chips, LANES)
        row_ffn = shapes(n_tp, 1, ffn)
        scratch = ([low(*big)] * 9 + [heads4, heads4, low(n_tp, width, dim)] + [shapes(*big)] * 2
                   + [shapes(n_chips, n_tile, dim), shapes(2, n_tile, dim), low(n_tp, seqs, p_len, n3)]
                   + [shapes(seq, width)] * 5 + [shapes(seqs, seq, LANES), stat, stat, shapes(n_tp, 1, n3), row_ffn, row_ffn, row_ffn]
                   + [shapes(n_tp, *b_qkv.shape), tile8, late, late, shapes(8, dim), mate, mate, shapes(6 * n_tp, LANES)]
                   + [low(tok, ffn)] + plain)
        outs = pl.pallas_call(
            kernel, name='layer', out_shape=out_shape, in_specs=[ANY] * 16, out_specs=[ANY] * len(out_shape),
            scratch_shapes=[pltpu.VMEM(v.shape, v.dtype) for v in scratch]
            + [sem(91), sem(91), sem(30), sem(20), sem(12), pltpu.SemaphoreType.REGULAR],
            compiler_params=pltpu.CompilerParams(collective_id=0, has_side_effects=True, vmem_limit_bytes=VMEM_LIMIT),
        )(flat(x_in), flat(grad_y), w_qkv.transpose(0, 2, 3, 1).reshape(n3, dim), b_qkv, w_out.reshape(width, dim),
          w_up, line(b_up), w_down, *plain)

        def finish(*refs):
            src, (v_ref, b_ref), out, (bq_o, bu_o), v_o = refs[:6], refs[6:8], refs[8:14], refs[14:16], refs[16:]
            for a, b in zip(src, out):
                b[...] = a[...]
            for i in range(3):
                for h in range(heads):
                    bq_o[i, h:h + 1, :] = b_ref[i:i + 1, h * hd:(h + 1) * hd]
            unfold(b_ref, 3, bu_o)
            for r, ref in enumerate(v_o):
                unfold(v_ref, r * n_tp, ref)

        large = [low(*big)] * 2 + [shapes(dim, ffn), shapes(ffn, dim), shapes(n3, dim), shapes(width, dim)]
        small = [shapes(*b_qkv.shape), shapes(1, ffn)] + [shapes(1, dim)] * 6
        moving = [pl.BlockSpec((v.shape[0] // n_chips, v.shape[1]), lambda i: (i, 0)) for v in large]
        fixed = lambda vs: [pl.BlockSpec(v.shape, lambda i, n=len(v.shape): (0,) * n) for v in vs]
        res = pl.pallas_call(
            finish, name='finish', out_shape=large + small, grid=(n_chips,), in_specs=moving + fixed(outs[6:8]),
            out_specs=moving + fixed(small), compiler_params=pltpu.CompilerParams(vmem_limit_bytes=VMEM_LIMIT),
        )(*outs[:8])
        y_out, grad_x, grad_w_up, grad_w_down, gq, go, grad_b_qkv, grad_b_up = res[:8]
        v = [t.reshape(dim) for t in res[8:]]
        return (y_out.reshape(x_in.shape), grad_x.reshape(x_in.shape), v[0], v[1], gq.reshape(3, heads, hd, dim).transpose(0, 3, 1, 2),
                grad_b_qkv, go.reshape(heads, hd, dim), v[2], v[3], v[4], grad_w_up, grad_b_up.reshape(ffn), grad_w_down, v[5])

    return jax.shard_map(device_step, mesh=mesh, in_specs=in_specs, out_specs=out_specs, check_vma=False)
```

profile of v0, /device:TPU:113, one launch (start us, length us, event | category | flops | bytes accessed | tf_op | source)
XLA Modules:
  0.0 367.2 jit_solution(7180292052319676492)
XLA Ops:
  0.7 358.4 %layer.1 = (bf16[1024,1024]{1,0:T(8,128)(2,1)}, bf16[1024,1024]{1,0:T(8,128)(2,1)}, f32[1024,512]{1,0:T(8,128)}, f32[512,1024]{1,0:T(8,128)}, f32[384,1024]{1,0:...) custom-call(bf16[1024,1024]{1,0:T(8,128)(2,1)} %bitcast.26, ...), custom_call_target="tpu_custom_call" | custom-call | tf_op jit(solution)/shard_map/layer/pallas_call | solution.py:758
  359.1 7.9 %finish.1 = (bf16[1024,1024]{1,0:T(8,128)(2,1)}, bf16[1024,1024]{1,0:T(8,128)(2,1)}, f32[1024,512]{1,0:T(8,128)}, f32[512,1024]{1,0:T(8,128)}, f32[384,1024]{1,0...) custom-call(bf16[1024,1024]{1,0:T(8,128)(2,1)} %get-tuple-element.36, ...), custom_call_target="tpu_custom_call" | custom-call | tf_op jit(solution)/shard_map/finish/pallas_call | solution.py:781
where the time goes:
time: 367 us
  Pallas kernels  366 us (100%)
    pallas_call x1, Pallas kernels, device_step(): pl.pallas_call(kernel, name='layer', out_shape=out_shape, in_specs=[ANY]...  358 us
    pallas_call x1, Pallas kernels, device_step(): pl.pallas_call(finish, name='finish', out_shape=large + small, grid=(n_ch...  7.93 us

commit v1 on v0

--- a/solution.py
+++ b/solution.py
@@ -1,4 +1,5 @@
 import functools
+import itertools
 
 import jax
 import jax.numpy as jnp
@@ -132,11 +133,14 @@
         self.add(name + 'r', src, here, via)
         self.add(name + 'l', here, other, 0, 1)
 
-    def exchange(self, name, src, dst, rows):
+    def exchange(self, name, src, dst, rows, stage=None):
         me = lax.axis_index('tp')
         for core in BOTH:
             for chip in (PAIR, CROSS, FAR, 0):
-                if chip + core:
+                if chip == FAR and stage is not None:
+                    self.add(name + '_by', lambda k=core: src.at[span(self.peer(FAR, k), rows)], lambda k=core: stage.at[k], PAIR)
+                    self.add(name + '_on', lambda k=core: stage.at[k], lambda: dst.at[span(self.peer(PAIR), rows)], CROSS, core)
+                elif chip + core:
                     self.add(name, lambda c=chip, k=core: src.at[span(self.peer(c, k), rows)], lambda: dst.at[span(me, rows)], chip, core)
         self.add_local(name + '_own', lambda: src.at[span(me, rows)], lambda: dst.at[span(me, rows)])
 
@@ -191,7 +195,7 @@
             it = iter(refs)
             take = lambda n: [next(it) for _ in range(n)]
             (x_ref, dy_ref, wq_ref, bq_ref, wo_ref, wu_ref, bu_ref, wd_ref), plain = take(8), take(8)
-            y_out, gx_out, g_up, g_down, g_q, g_o, g_vec, g_b, wq, wu, wd, q_hbm, k_hbm, v_hbm, act_hbm, slope_hbm = take(16)
+            y_out, gx_out, g_up, g_down, g_q, g_o, g_vec, g_b, wq, wu, wd, q_hbm, k_hbm, v_hbm, act_hbm, slope_hbm, stage = take(17)
             p_at, got_at, sum_at, early_at, last_at, x_dn, x_up, p_dn, p_up, r_dn, r_up = take(11)
             x, h1, dy, x1, h2, dx1b, h2p, dyp, y, o4, do4, wo, acc, acc2, p_rcv, p_snd, d4 = take(17)
             dq_acc, dk_acc, dv_acc, cos_t, sin_t, ok, m_st, l_st, b_att, b_ffn, u_all, gb, b_all, b8, late, late_in, vec, mate, mate_in, v_own = take(20)
@@ -214,7 +218,7 @@
                 net.gather_far(f'd{i}', lambda i=i: wd.at[2 * CROSS, pl.ds(i * quarter, quarter)], lambda m=mine: m(0), lambda m=mine: m(1), PAIR)
             net.exchange('x', x_ref, x, chunk)
             net.multicast('dy', dy_ref, dy, dyp, chunk)
-            net.exchange('y', y, y_out, chunk)
+            net.exchange('y', y, y_out, chunk, stage)
             net.exchange('gx', h1, gx_out, chunk)
             for chip in range(n_chips):
                 for core in BOTH:
@@ -438,8 +442,8 @@
 
             def gelu(pre):
                 erf_term = lax.erf(pre * INV_SQRT2)
-                act = (0.5 * pre * (1.0 + erf_term)).astype(BF16)
-                return act, 0.5 * (1.0 + erf_term) + pre * jnp.exp(-0.5 * pre * pre) * INV_SQRT_2PI
+                phi = 0.5 * (1.0 + erf_term)
+                return (pre * phi).astype(BF16), phi + pre * jnp.exp(-0.5 * pre * pre) * INV_SQRT_2PI
 
             cols = lambda f: pl.BlockSpec((tok, ffn), lambda s: (0, f(s)))
             wu_spec, wd_spec = functools.partial(slot3, dim, ffn), functools.partial(slot3, ffn, dim)
@@ -582,7 +586,7 @@
 
             loop_rows(tok, 2 * chunk, y_rows)
             vec[...] = jnp.zeros_like(vec)
-            net.start('y', 'y_own')
+            net.start('y', 'y_by', 'y_own')
             net.sent('d0l', 'd1l')
 
             @pl.loop(0, tok // (2 * chunk))
@@ -605,7 +609,7 @@
                 step = ps.index[0]
                 g = order(step)
                 hooks(step, {2: lambda: (stored(0), net.start('at_relay0', 'at_relay1')),
-                             4: lambda: (stored(1), net.start('at_early')), 6: lambda: (stored(2), pass_on(0, 0)), 7: lambda: pass_on(0, 2)})
+                             3: lambda: (net.got('y_by'), net.start('y_on')), 4: lambda: (stored(1), net.start('at_early')), 6: lambda: (stored(2), pass_on(0, 0)), 7: lambda: pass_on(0, 2)})
                 pair_go(step)
                 b8[g] = jnp.zeros_like(b8[0])
                 fold(gb[g], b8.at[g], 3)
@@ -690,7 +694,7 @@
             pass_on(1, 2)
             net.start('gx', 'gx_own')
 
-            net.sent('y')
+            net.sent('y', 'y_by')
             net.done('y_own')
             pair_begin()
             grads(0, 2, p_dn, lambda: None)
@@ -722,9 +726,9 @@
             for rows, out, n in ((pl.ds(0, n3), g_q, n3), (pl.ds(n3, width), g_o, width)):
                 total((p_at.at[0, rows], early_at.at[rows], last_at.at[rows]), out, (n // 2, dim), by_row)
             for name in net.copies:
-                if name not in ('load', 'store', 'own', 'write', 'gx', 'y', 'd0l', 'd1l') and not name.endswith(('_own', '_load', '_store')):
+                if name not in ('load', 'store', 'own', 'write', 'gx', 'y', 'y_by', 'd0l', 'd1l') and not name.endswith(('_own', '_load', '_store')):
                     net.sent(name)
-            net.got('y', 'final')
+            net.got('y', 'y_on', 'final')
             net.start('write')
             net.done('gx_own', 'write')
             net.got('gx')
@@ -742,7 +746,7 @@
         weights = [low(n_tp, n3, dim), low(n_tp, dim, ffn), low(n_tp, ffn, dim)]
         tiles = [shapes(n_chips, n_tile, dim)] + [shapes(n_tile, dim)] * 10
         out_shape = ([low(*big)] * 2 + [shapes(dim, ffn), shapes(ffn, dim), shapes(n3, dim), shapes(width, dim), shapes(6 * n_tp, LANES), shapes(8, LANES)] + weights
-                     + [low(n_tp, n_tp, seqs, p_len, width)] * 3 + [low(tok, n_tp * ffn), shapes(tok, n_tp * ffn)] + tiles)
+                     + [low(n_tp, n_tp, seqs, p_len, width)] * 3 + [low(tok, n_tp * ffn), shapes(tok, n_tp * ffn), low(2, chunk, dim)] + tiles)
         plain = [pad_mask] + [line(v) for v in (ln1_gain, ln1_bias, b_out, ln2_gain, b_down, ln2_bias)] + [freq]
         heads4 = low(n_tp, seqs, p_len, n_tp * width)
         stat = shapes(n_tp, seqs, heads, seq)
@@ -758,13 +762,15 @@
         outs = pl.pallas_call(
             kernel, name='layer', out_shape=out_shape, in_specs=[ANY] * 16, out_specs=[ANY] * len(out_shape),
             scratch_shapes=[pltpu.VMEM(v.shape, v.dtype) for v in scratch]
-            + [sem(91), sem(91), sem(30), sem(20), sem(12), pltpu.SemaphoreType.REGULAR],
+            + [sem(93), sem(93), sem(30), sem(20), sem(12), pltpu.SemaphoreType.REGULAR],
             compiler_params=pltpu.CompilerParams(collective_id=0, has_side_effects=True, vmem_limit_bytes=VMEM_LIMIT),
         )(flat(x_in), flat(grad_y), w_qkv.transpose(0, 2, 3, 1).reshape(n3, dim), b_qkv, w_out.reshape(width, dim),
           w_up, line(b_up), w_down, *plain)
 
         def finish(*refs):
-            src, (v_ref, b_ref), out, (bq_o, bu_o), v_o = refs[:6], refs[6:8], refs[8:14], refs[14:16], refs[16:]
+            it = iter(refs)
+            n = len(large)
+            src, (v_ref, b_ref), out, (bq_o, bu_o), v_o = (list(itertools.islice(it, k)) for k in (n, 2, n, 2, n))
             for a, b in zip(src, out):
                 b[...] = a[...]
             for i in range(3):

time: 367 us -> 368 us (level)
  no operation moved by 1% of the time
where the time goes in v1:
time: 368 us; the launch traced here: 367 us
  Pallas kernels  366 us (99%)
    pallas_call x1, Pallas kernels, device_step(): pl.pallas_call(kernel, name='layer', out_shape=out_shape, in_specs=[ANY]...  358 us
    pallas_call x1, Pallas kernels, device_step(): pl.pallas_call(finish, name='finish', out_shape=large + small, grid=(n_ch...  7.93 us

profile of v1, /device:TPU:113, one launch (start us, length us, event | category | flops | bytes accessed | tf_op | source)
XLA Modules:
  0.0 367.2 jit_solution(12807493694699505528)
XLA Ops:
  0.7 358.4 %layer.1 = (bf16[1024,1024]{1,0:T(8,128)(2,1)}, bf16[1024,1024]{1,0:T(8,128)(2,1)}, f32[1024,512]{1,0:T(8,128)}, f32[512,1024]{1,0:T(8,128)}, f32[384,1024]{1,0:...) custom-call(bf16[1024,1024]{1,0:T(8,128)(2,1)} %bitcast.26, ...), custom_call_target="tpu_custom_call" | custom-call | tf_op jit(solution)/shard_map/layer/pallas_call | solution.py:762
  359.1 7.9 %finish.1 = (bf16[1024,1024]{1,0:T(8,128)(2,1)}, bf16[1024,1024]{1,0:T(8,128)(2,1)}, f32[1024,512]{1,0:T(8,128)}, f32[512,1024]{1,0:T(8,128)}, f32[384,1024]{1,0...) custom-call(bf16[1024,1024]{1,0:T(8,128)(2,1)} %get-tuple-element.36, ...), custom_call_target="tpu_custom_call" | custom-call | tf_op jit(solution)/shard_map/finish/pallas_call | solution.py:787

commit v2 on v0

--- a/solution.py
+++ b/solution.py
@@ -438,8 +438,8 @@
 
             def gelu(pre):
                 erf_term = lax.erf(pre * INV_SQRT2)
-                act = (0.5 * pre * (1.0 + erf_term)).astype(BF16)
-                return act, 0.5 * (1.0 + erf_term) + pre * jnp.exp(-0.5 * pre * pre) * INV_SQRT_2PI
+                phi = 0.5 * (1.0 + erf_term)
+                return (pre * phi).astype(BF16), phi + pre * jnp.exp(-0.5 * pre * pre) * INV_SQRT_2PI
 
             cols = lambda f: pl.BlockSpec((tok, ffn), lambda s: (0, f(s)))
             wu_spec, wd_spec = functools.partial(slot3, dim, ffn), functools.partial(slot3, ffn, dim)
@@ -478,7 +478,7 @@
             def pair_gelu(rows, w_u, slot):
                 return gelu(mm(h2p[rows, :], w_u, NN) + b_ffn[slot])
 
-            def grads(chip, at, x_ref, between):
+            def grads(chip, at, x_ref, between, arrive):
                 f = lambda s: 2 * chip + 1 - s
                 copy = to_partner(0, at, n_tp + at)
 
@@ -490,6 +490,7 @@
 
                 def second(ps, w_u):
                     s = ps.index[0]
+                    pl.when(s == 0)(lambda: arrive())
                     pl.when(s == 1)(lambda: copy.start())
                     rows = pl.ds(half, half)
                     act_p[rows, :] = pair_gelu(rows, w_u[0], f(s))[0]
@@ -545,7 +546,7 @@
             net.got('ul')
             mlp_up(2, lambda s: s + FAR0, {})
             net.got('h0')
-            grads(CROSS, 0, x_dn, lambda: (net.got('dc'), net.start('dg', 'd0r', 'd1r'), net.got('h1')))
+            grads(CROSS, 0, x_dn, lambda: (net.got('dc'), net.start('dg', 'd0r', 'd1r')), lambda: net.got('h1'))
             net.start('dn_x')
             net.got('dg')
 
@@ -693,7 +694,7 @@
             net.sent('y')
             net.done('y_own')
             pair_begin()
-            grads(0, 2, p_dn, lambda: None)
+            grads(0, 2, p_dn, lambda: None, lambda: None)
             mlp(2, lambda s: 1 - s, False, {}, (2, p_up, None))
             keep(3, p_up).wait()
 

time: 367 us -> 368 us (level)
  no operation moved by 1% of the time
where the time goes in v2:
time: 368 us; the launch traced here: 367 us
  Pallas kernels  366 us (99%)
    pallas_call x1, Pallas kernels, device_step(): pl.pallas_call(kernel, name='layer', out_shape=out_shape, in_specs=[ANY]...  358 us
    pallas_call x1, Pallas kernels, device_step(): pl.pallas_call(finish, name='finish', out_shape=large + small, grid=(n_ch...  7.93 us

profile of v2, /device:TPU:113, one launch (start us, length us, event | category | flops | bytes accessed | tf_op | source)
XLA Modules:
  0.0 367.2 jit_solution(10164406138004678024)
XLA Ops:
  0.7 358.4 %layer.1 = (bf16[1024,1024]{1,0:T(8,128)(2,1)}, bf16[1024,1024]{1,0:T(8,128)(2,1)}, f32[1024,512]{1,0:T(8,128)}, f32[512,1024]{1,0:T(8,128)}, f32[384,1024]{1,0:...) custom-call(bf16[1024,1024]{1,0:T(8,128)(2,1)} %bitcast.26, ...), custom_call_target="tpu_custom_call" | custom-call | tf_op jit(solution)/shard_map/layer/pallas_call | solution.py:759
  359.1 7.9 %finish.1 = (bf16[1024,1024]{1,0:T(8,128)(2,1)}, bf16[1024,1024]{1,0:T(8,128)(2,1)}, f32[1024,512]{1,0:T(8,128)}, f32[512,1024]{1,0:T(8,128)}, f32[384,1024]{1,0...) custom-call(bf16[1024,1024]{1,0:T(8,128)(2,1)} %get-tuple-element.36, ...), custom_call_target="tpu_custom_call" | custom-call | tf_op jit(solution)/shard_map/finish/pallas_call | solution.py:782

commit v3 on v2

--- a/solution.py
+++ b/solution.py
@@ -560,16 +560,28 @@
             for slot in (FAR0, FAR1):
                 gb[slot] = jnp.zeros_like(gb[slot])
 
+            def y_rows(rows):
+                y[rows, :] = (x1[rows, :].astype(F32) + (acc[rows, :] + bias_d[...])).astype(BF16)
+
             def far_step(ps, w_u, act_ref, slope_ref):
                 part, core = ps.index
                 hooks(2 * part + core, {0: lambda: (net.got('d0r'), net.start('d0l')), 1: lambda: net.got('d0l'),
                                         2: lambda: (net.got('d1r'), net.start('d1l')), 3: lambda: net.got('d1l')})
                 w_d = dx1b[pl.ds(pl.multiple_of(core * ffn + part * quarter, quarter), quarter), :]
 
+                def forward(rows):
+                    acc[rows, :] += mm(act_ref[rows, :], w_d, NN)
+
+                loop_rows(tok, half, forward)
+
+                @pl.when(part + core == FAR)
+                def _():
+                    loop_rows(tok, chunk, y_rows)
+                    net.start('y', 'y_own')
+
                 def body(rows):
                     d_pre = mm(dy[rows, :], w_d, NT) * slope_ref[rows, :]
                     gb[FAR0 + core, :, span(part, quarter)] += col_sum(d_pre)
-                    acc[rows, :] += mm(act_ref[rows, :], w_d, NN)
                     acc2[rows, :] += mm(d_pre.astype(BF16), w_u[0], NT)
 
                 loop_rows(tok, half, body)
@@ -578,12 +590,7 @@
             pipe(far_step, grid=(len(BOTH),) * len(BOTH), in_specs=[pl.BlockSpec((1, dim, quarter), lambda part, core: (FAR0 + core, 0, part)), narrow, narrow])(
                 wu, act_hbm, slope_hbm)
 
-            def y_rows(rows):
-                y[rows, :] = (x1[rows, :].astype(F32) + (acc[rows, :] + bias_d[...])).astype(BF16)
-
-            loop_rows(tok, 2 * chunk, y_rows)
             vec[...] = jnp.zeros_like(vec)
-            net.start('y', 'y_own')
             net.sent('d0l', 'd1l')
 
             @pl.loop(0, tok // (2 * chunk))

time: 368 us -> 372 us (1.011)
  Pallas kernels: 366 us -> 371 us
    pallas_call x1, Pallas kernels: 358 us -> 363 us  [device_step(): pl.pallas_call(kernel, name='layer', out_shape=out_shape, in_specs=[ANY]...]
where the time goes in v3:
time: 372 us
  Pallas kernels  371 us (100%)
    pallas_call x1, Pallas kernels, device_step(): pl.pallas_call(kernel, name='layer', out_shape=out_shape, in_specs=[ANY]...  363 us
    pallas_call x1, Pallas kernels, device_step(): pl.pallas_call(finish, name='finish', out_shape=large + small, grid=(n_ch...  7.93 us

profile of v3, /device:TPU:113, one launch (start us, length us, event | category | flops | bytes accessed | tf_op | source)
XLA Modules:
  0.0 371.6 jit_solution(13543456092451034510)
XLA Ops:
  0.7 362.8 %layer.1 = (bf16[1024,1024]{1,0:T(8,128)(2,1)}, bf16[1024,1024]{1,0:T(8,128)(2,1)}, f32[1024,512]{1,0:T(8,128)}, f32[512,1024]{1,0:T(8,128)}, f32[384,1024]{1,0:...) custom-call(bf16[1024,1024]{1,0:T(8,128)(2,1)} %bitcast.26, ...), custom_call_target="tpu_custom_call" | custom-call | tf_op jit(solution)/shard_map/layer/pallas_call | solution.py:766
  363.5 7.9 %finish.1 = (bf16[1024,1024]{1,0:T(8,128)(2,1)}, bf16[1024,1024]{1,0:T(8,128)(2,1)}, f32[1024,512]{1,0:T(8,128)}, f32[512,1024]{1,0:T(8,128)}, f32[384,1024]{1,0...) custom-call(bf16[1024,1024]{1,0:T(8,128)(2,1)} %get-tuple-element.36, ...), custom_call_target="tpu_custom_call" | custom-call | tf_op jit(solution)/shard_map/finish/pallas_call | solution.py:789
